TPU v7x, 32 devices: a 4x4x1 block of a 4x4x8 slice. The times are simulated.
32 devices in a mesh: dp: 1 (over z), tp: 4 (over y), sp: 8 (over x, core).
Axes of the slice: x: 4, y: 4, z: 1, core: 2. Of those that a mesh axis runs over, the one named last changes fastest.
The devices are a block of a 4x4x8 slice.
Arguments:
- hidden: bfloat16 [16, 18432], P('dp')
- ln_gain: bfloat16 [18432], replicated
- ln_bias: bfloat16 [18432], replicated
- w_q: bfloat16 [18432, 18432], P(None, 'tp')
- w_k: bfloat16 [18432, 1536], P(None, 'tp')
- w_v: bfloat16 [18432, 1536], P(None, 'tp')
- w_o: bfloat16 [18432, 18432], P('tp')
- k_cache: bfloat16 [16, 1024, 8, 192], P('dp', 'sp', 'tp')
- v_cache: bfloat16 [16, 1024, 8, 192], P('dp', 'sp', 'tp')
- lengths: int32 [16], P('dp')
Outputs:
- output 1: bfloat16 [16, 18432], P('dp')
- output 2: bfloat16 [16, 8, 192], P('dp', 'tp')
- output 3: bfloat16 [16, 8, 192], P('dp', 'tp')
All inputs are finite; a program needn't handle non-finite values.
Results may differ from a plain program's by a relative error of at most 0.00424821.
Values sent between devices are 32-bit elements.
A program may use at most 768 MiB of HBM per device.

v0:
```python
import jax
import jax.numpy as jnp
from jax import lax
from jax.sharding import PartitionSpec as P, NamedSharding


def norm_one_plus(hidden, ln_gain, ln_bias):
    wide = hidden.astype(jnp.float32)
    row_mean = jnp.mean(wide, axis=-1, keepdims=True)
    centred = wide - row_mean
    row_var = jnp.mean(centred * centred, axis=-1, keepdims=True)
    scaled = centred * lax.rsqrt(row_var + 1e-5)
    return (scaled * (1.0 + ln_gain.astype(jnp.float32)) + ln_bias.astype(jnp.float32)).astype(jnp.bfloat16)


def rotate_first(head_vecs, rot_pos, rot_dim):
    half_rot = rot_dim // 2
    inv_freq = 10000.0 ** (-2.0 * jnp.arange(half_rot, dtype=jnp.float32) / rot_dim)
    rot_angle = rot_pos.astype(jnp.float32)[..., None] * inv_freq
    cos_part = jnp.cos(rot_angle)
    sin_part = jnp.sin(rot_angle)
    lead_part = head_vecs[..., :half_rot]
    tail_part = head_vecs[..., half_rot:rot_dim]
    return jnp.concatenate([lead_part * cos_part - tail_part * sin_part, tail_part * cos_part + lead_part * sin_part, head_vecs[..., rot_dim:]], axis=-1)


def solution(mesh):
    def local_step(hidden, ln_gain, ln_bias, w_q, w_k, w_v, w_o, k_cache, v_cache, lengths):
        batch_rows, seq_local, kv_local, head_dim = k_cache.shape
        group_size = w_q.shape[1] // (head_dim * kv_local)
        rot_dim = head_dim // 2
        score_scale = head_dim ** -0.5
        normed = norm_one_plus(hidden, ln_gain, ln_bias)
        q_proj = jnp.dot(normed, w_q, preferred_element_type=jnp.float32).reshape(batch_rows, kv_local, group_size, head_dim)
        queries = rotate_first(q_proj, lengths[:, None, None], rot_dim).astype(jnp.bfloat16)
        k_proj = jnp.dot(normed, w_k, preferred_element_type=jnp.float32).reshape(batch_rows, kv_local, head_dim)
        k_new = rotate_first(k_proj, lengths[:, None], rot_dim).astype(jnp.bfloat16)
        v_new = jnp.dot(normed, w_v, preferred_element_type=jnp.float32).astype(jnp.bfloat16).reshape(batch_rows, kv_local, head_dim)
        block_index = lax.axis_index('sp')
        positions = block_index * seq_local + jnp.arange(seq_local)
        valid = positions[None, :] < lengths[:, None]
        scores = jnp.einsum('bkgd,bskd->bkgs', queries, k_cache, preferred_element_type=jnp.float32) * score_scale
        scores = jnp.where(valid[:, None, None, :], scores, -jnp.inf)
        owner = (lengths // seq_local) == block_index
        self_score = jnp.einsum('clhe,cle->clh', queries, k_new, preferred_element_type=jnp.float32) * score_scale
        self_score = jnp.where(owner[:, None, None], self_score, -jnp.inf)
        block_max = jnp.maximum(jnp.max(scores, axis=-1), self_score)
        safe_max = jnp.where(jnp.isfinite(block_max), block_max, 0.0)
        weights = jnp.exp(scores - safe_max[..., None])
        self_weight = jnp.exp(self_score - safe_max)
        weight_sum = jnp.sum(weights, axis=-1) + self_weight
        weighted = jnp.einsum('bkgs,bskd->bkgd', weights.astype(jnp.bfloat16), v_cache, preferred_element_type=jnp.float32)
        weighted = weighted + self_weight[..., None] * v_new.astype(jnp.float32)[:, :, None, :]
        packed = jnp.concatenate([weighted, block_max[..., None], weight_sum[..., None]], axis=-1)
        gathered = lax.all_gather(packed, 'sp', axis=0)
        all_max = gathered[..., head_dim]
        global_max = jnp.max(all_max, axis=0)
        factor = jnp.exp(all_max - global_max)
        total = jnp.sum(gathered[..., head_dim + 1] * factor, axis=0)
        context = jnp.sum(gathered[..., :head_dim] * factor[..., None], axis=0) / total[..., None]
        context = context.astype(jnp.bfloat16).reshape(batch_rows, kv_local * group_size * head_dim)
        partial_out = jnp.dot(context, w_o, preferred_element_type=jnp.float32)
        summed = lax.psum(partial_out, 'tp')
        out = (hidden.astype(jnp.float32) + summed).astype(jnp.bfloat16)
        return out, k_new, v_new

    row_spec = P('dp', None)
    cache_spec = P('dp', 'sp', 'tp', None)
    head_spec = P('dp', 'tp', None)
    return jax.shard_map(local_step, mesh=mesh, in_specs=(row_spec, P(None), P(None), P(None, 'tp'), P(None, 'tp'), P(None, 'tp'), P('tp', None), cache_spec, cache_spec, P('dp')), out_specs=(row_spec, head_spec, head_spec), check_vma=False)
```

profile of v0, /device:TPU:97, one launch (start us, length us, event | category | flops | bytes accessed | tf_op | source)
XLA Modules:
  0.0 222.9 jit_solution(3448468106703743511)
XLA Ops:
  7.2 0.0 copy-start
  7.2 0.0 copy-start.1
  7.2 0.1 all-gather.3.cloned.1.call-start
  7.3 0.8 convert_element_type.48
  8.1 1.3 convert_reduce_fusion
  9.5 1.4 fusion.3
  10.9 0.8 convert_add_fusion.1
  11.6 0.8 convert_element_type.46
  12.4 0.0 copy-done.1
  12.4 6.1 %fusion.19 = f32[16,384]{1,0:T(8,128)S(1)} fusion(bf16[18432,384]{1,0:T(8,128)(2,1)} %param.14, bf16[16,18432]{1,0:T(8,128)(2,1)S(1)} %copy-done.1, f32[18432]{0:T(1024)S(1)} %convert_element_type.46, f32[18432]{0:T(1024)S(1)} %convert_add_fusion.1, f32[16]{0:T(128)S(1)} %add_rsqrt_fusion, f32[16]{0:T(128)S(1)} %broadcast_multiply_fusion), kind=kOutput, calls=%fused_computation.57 | convolution fusion | flops 228261888 | bytes 14917760 | tf_op jit(solution)/shard_map/dot_general | solution.py:36
  18.5 0.1 reshape.194
  18.6 0.1 slice.65
  18.7 52.9 %fusion.21 = f32[16,4608]{1,0:T(8,128)S(1)} fusion(bf16[18432,4608]{1,0:T(8,128)(2,1)} %param.13, bf16[16,18432]{1,0:T(8,128)(2,1)S(1)} %copy-done.1, f32[18432]{0:T(1024)S(1)} %convert_element_type.46, f32[18432]{0:T(1024)S(1)} %convert_add_fusion.1, f32[16]{0:T(128)S(1)} %add_rsqrt_fusion, f32[16]{0:T(128)S(1)} %broadcast_multiply_fusion), kind=kOutput, calls=%fused_computation.58 | convolution fusion | flops 2719678464 | bytes 170901632 | tf_op jit(solution)/shard_map/dot_general | solution.py:34
  71.6 0.2 reshape.193
  71.9 0.1 slice.64
  72.0 0.1 multiply_cosine_fusion
  72.1 0.1 subtract_convert_fusion.1
  72.2 0.1 subtract_convert_fusion
  72.3 0.0 copy-done.3
  72.4 0.1 broadcast_compare_fusion
  72.5 6.1 %convolution_convert_fusion = bf16[16,384]{1,0:T(8,128)(2,1)S(1)} fusion(bf16[18432,384]{1,0:T(8,128)(2,1)} %param.15, bf16[16,18432]{1,0:T(8,128)(2,1)S(1)} %copy-done.1, f32[18432]{0:T(1024)S(1)} %convert_element_type.46, f32[18432]{0:T(1024)S(1)} %convert_add_fusion.1, f32[16]{0:T(128)S(1)} %add_rsqrt_fusion, f32[16]{0:T(128)S(1)} %broadcast_multiply_fusion), kind=kOutput, calls=%fused_computation.19 | convolution fusion | flops 228268032 | bytes 14905472 | tf_op jit(solution)/shard_map/dot_general | solution.py:38
  78.6 0.1 reshape.195
  78.7 0.1 fusion.32
  78.8 0.3 fusion.13
  79.1 2.1 fusion.23
  81.2 0.1 is-finite_select_fusion
  81.3 0.3 fusion.9
  81.6 0.1 add_bitcast_fusion
  81.7 0.3 copy.51
  82.1 0.3 copy.50
  82.4 1.0 convolution_add_fusion
  83.3 0.2 pad_maximum_fusion
  83.5 1.1 copy.52
  84.6 0.1 all-gather.3.cloned.1.call-update
  84.7 0.2 all-reduce.2.cloned.1.call-start
  84.9 29.1 %all-gather.3.cloned.1.call-done = f32[128,2,12,194]{3,1,2,0:T(2,128)} async-done(((f32[16,2,12,194]{3,1,2,0:T(2,128)}), f32[128,2,12,194]{3,1,2,0:T(2,128)}) %all-gather.3.cloned.1.call-update) | async-done | bytes 2383888 | tf_op jit(solution)/shard_map/all_gather | solution.py:55
  114.0 2.9 %copy.53 = f32[128,2,12,194]{3,0,2,1:T(8,128)S(1)} copy(f32[128,2,12,194]{3,1,2,0:T(2,128)} %all-gather.3.cloned.1.call-done) | data formatting | bytes 4767744 | tf_op jit(solution)/shard_map/all_gather | solution.py:55
  117.0 0.6 slice_reduce_fusion.2
  117.5 2.2 slice_reduce_fusion.1
  119.7 0.5 fusion
  120.2 0.1 divide_convert_fusion
  120.4 0.1 copy.54
  120.5 0.2 convert_element_type.53
  120.7 53.5 %fusion.24 = f32[16,18432]{1,0:T(8,128)} fusion(bf16[16,4608]{1,0:T(8,128)(2,1)S(1)} %convert_element_type.53, bf16[4608,18432]{1,0:T(8,128)(2,1)} %param.16), kind=kOutput, calls=%fused_computation.60 | convolution fusion | flops 2717908992 | bytes 171196416 | tf_op jit(solution)/shard_map/dot_general | solution.py:62
  174.2 0.1 all-reduce.2.cloned.1.call-update
  174.3 0.7 pad_maximum_fusion.4
  175.0 38.9 %all-reduce.2.cloned.1.call-done = f32[16,18432]{1,0:T(8,128)} async-done(((f32[16,18432]{1,0:T(8,128)}), f32[16,18432]{1,0:T(8,128)}) %all-reduce.2.cloned.1.call-update) | async-done | bytes 1179664 | tf_op jit(solution)/shard_map/psum | solution.py:63
  213.9 2.2 fusion.7
  (11 shorter events, 0.1 us)
Async XLA Ops:
  7.2 75.2 %copy-start = (bf16[16,128,2,192]{1,3,2,0:T(8,128)(2,1)S(1)}, bf16[16,128,2,192]{1,3,2,0:T(8,128)(2,1)}, u32[]{:S(2)}) copy-start(bf16[16,128,2,192]{1,3,2,0:T(8,128)(2,1)} %param.18) | copy-start | bytes 4718596
  7.2 5.2 %copy-start.1 = (bf16[16,18432]{1,0:T(8,128)(2,1)S(1)}, bf16[16,18432]{1,0:T(8,128)(2,1)}, u32[]{:S(2)}) copy-start(bf16[16,18432]{1,0:T(8,128)(2,1)} %param.10) | copy-start | bytes 1769476
  7.2 106.8 %all-gather.3.cloned.1.call-start = ((), (), s32[]{:S(2)}) async-start(), calls=%async_computation.1 | async-start | bytes 3538944 | tf_op jit(solution)/shard_map/all_gather | solution.py:55
  71.6 0.7 copy-start.3
  78.7 2.6 %copy-start.2 = (bf16[16,2,192]{2,1,0:T(2,128)(2,1)}, bf16[16,2,192]{2,1,0:T(2,128)(2,1)S(1)}, u32[]{:S(2)}) copy-start(bf16[16,2,192]{2,1,0:T(2,128)(2,1)S(1)} %reshape.195) | copy-start | bytes 36868
  84.7 129.2 %all-reduce.2.cloned.1.call-start = ((), (), s32[]{:S(2)}) async-start(), calls=%async_computation | async-start | bytes 2359296 | tf_op jit(solution)/shard_map/psum | solution.py:63
Sparse Core Ops, SparseCore 0:
  84.8 29.2 all-gather.2
  174.4 39.4 all-reduce.1
where the time goes:
time: 224 us; the launch traced here: 223 us
  matrix products  122 us (54%)
  waiting for transfers between devices  68.1 us (30%)
  between operations  14.3 us (6%)
  other arithmetic  12.7 us (6%)
  local copies, waits for them, and re-layouts  5.46 us (2%)
    dot_general x1, matrix products, local_step(): partial_out = jnp.dot(context, w_o, preferred_element_type=jnp.float32)  53.5 us
    dot_general x1, matrix products, local_step(): jnp.dot(normed, w_q, preferred_element_type=jnp.float32)  52.9 us
    psum x1, waiting for transfers between devices, local_step(): summed = lax.psum(partial_out, 'tp')  38.9 us
    all_gather x1, waiting for transfers between devices, local_step(): gathered = lax.all_gather(packed, 'sp', axis=0)  29.1 us
    dot_general x1, matrix products, local_step(): jnp.dot(normed, w_v, preferred_element_type=jnp.float32)  6.12 us
    dot_general x1, matrix products, local_step(): jnp.dot(normed, w_k, preferred_element_type=jnp.float32)  6.11 us
  transfers between devices with their start and end apart: 2, of which 2 were waited for; matrix products, arithmetic and copies ran while one was open for 0% of the time, Pallas kernels for 0%

commit v1 on v0

v1 whole, which is shorter than its diff:
```python
import functools

import jax
import jax.numpy as jnp
from jax import lax
from jax.experimental import pallas as pl
from jax.experimental.pallas import tpu as pltpu
from jax.sharding import PartitionSpec as P

F32 = jnp.float32
BF16 = jnp.bfloat16
MESH_ID = pl.DeviceIdType.MESH


def dot(a, b):
    return jnp.dot(a, b, preferred_element_type=F32)


def dot_t(a, b):
    return lax.dot_general(a, b, (((1,), (1,)), ((), ())), preferred_element_type=F32)


def rope(u, cos_t, sin_lo, sin_hi, half):
    width = u.shape[1]
    ahead = pltpu.roll(u, width - half, 1)
    behind = pltpu.roll(u, half, 1)
    return u * cos_t + ahead * sin_lo + behind * sin_hi


def kernel(cfg, hidden, gain, bias, w_q, w_k, w_v, w_o, k_t, v_t, lens, out, kv_out,
           hid_v, gb_raw, gb_f, h_v, len_s, wq_v, wkv_v, wo_v, kc_v, vc_v, k_snd, v_snd, k_rcv, v_rcv,
           qp, q_in, q_all, qh, kvp, kv_in, kv_all, kvn, score, ob, o_in, ctx_own, ctx_in, acc, rs_in,
           sem_small, sem_cache, sem_wq, sem_wkv, sem_wo,
           s_cx, r_cx, s_qd, r_qd, s_qg, r_qg, s_kd, r_kd, s_kg, r_kg, s_ke, r_ke,
           s_cr, r_cr, s_cg, r_cg, s_cf, r_cf, s_rs, r_rs, s_og, r_og, s_of, r_of):
    XN, TN, HD, G, KC, scale = cfg
    B, D = hidden.shape
    BH = B // 2
    SL = k_t.shape[3]
    KVN = k_t.shape[1]
    QW = w_q.shape[1] // XN
    KH = D // 2
    KVR = KH // (XN // 2)
    HB = QW // HD
    OW = D // (2 * XN)
    PW = OW // 2
    rot = HD // 2
    half = rot // 2
    strip = 2 * HD
    RB = HB * BH

    t = lax.axis_index('tp')
    s = lax.axis_index('sp')
    x = s // 2
    c = s % 2
    other = s + 1 - 2 * c
    xs = [(x + d) % XN for d in range(XN)]
    ts = [(t + d) % TN for d in range(TN)]
    partner = {'sp': other}

    def xpeer(d):
        return {'sp': 2 * xs[d] + c}

    def remote(src, dst, ss, rs, dev):
        return pltpu.make_async_remote_copy(src_ref=src, dst_ref=dst, send_sem=ss, recv_sem=rs, device_id=dev, device_id_type=MESH_ID)

    mine = pl.ds(pl.multiple_of(c * BH, BH), BH)
    theirs = pl.ds(pl.multiple_of((1 - c) * BH, BH), BH)

    c_hid = pltpu.make_async_copy(hidden, hid_v, sem_small.at[0])
    c_gain = pltpu.make_async_copy(gain, gb_raw.at[0], sem_small.at[1])
    c_bias = pltpu.make_async_copy(bias, gb_raw.at[1], sem_small.at[2])
    c_len = pltpu.make_async_copy(lens, len_s, sem_small.at[3])
    for cp in (c_hid, c_gain, c_bias, c_len):
        cp.start()
    c_cache = [pltpu.make_async_copy(k_t.at[theirs], kc_v.at[theirs], sem_cache.at[0]),
               pltpu.make_async_copy(v_t.at[theirs], vc_v.at[theirs], sem_cache.at[1]),
               pltpu.make_async_copy(k_t.at[mine], kc_v.at[mine], sem_cache.at[2]),
               pltpu.make_async_copy(v_t.at[mine], vc_v.at[mine], sem_cache.at[3])]
    qcol = pl.ds(pl.multiple_of(x * QW, 128), QW)
    NQ = KH // KC

    def wq_copy(i):
        return pltpu.make_async_copy(w_q.at[pl.ds(pl.multiple_of(c * KH + i * KC, KC), KC), qcol], wq_v.at[i], sem_wq.at[i])

    for i in range(2):
        wq_copy(i).start()
    c_cache[0].start()
    c_cache[1].start()
    for i in range(2, NQ):
        wq_copy(i).start()
    c_cache[2].start()
    c_cache[3].start()
    kvrow = pl.ds(pl.multiple_of(c * KH + (x % (XN // 2)) * KVR, KVR), KVR)
    c_wk = pltpu.make_async_copy(w_k.at[kvrow, :], wkv_v, sem_wkv.at[0])
    c_wv = pltpu.make_async_copy(w_v.at[kvrow, :], wkv_v, sem_wkv.at[0])

    @pl.when(x < XN // 2)
    def _():
        c_wk.start()

    @pl.when(x >= XN // 2)
    def _():
        c_wv.start()

    ocol = pl.ds(pl.multiple_of(s * OW, 128), OW)

    def wo_copy(d):
        return pltpu.make_async_copy(w_o.at[pl.ds(pl.multiple_of(xs[d] * QW, QW), QW), ocol], wo_v.at[d], sem_wo.at[d])

    for d in (0, 1, XN - 1) + tuple(range(2, XN - 1)):
        wo_copy(d).start()

    barrier = pltpu.get_barrier_semaphore()
    pl.semaphore_signal(barrier, inc=1, device_id=partner, device_id_type=MESH_ID)
    for dx in range(XN):
        for dt in range(TN):
            if dx or dt:
                pl.semaphore_signal(barrier, inc=1, device_id={'tp': ts[dt], 'sp': 2 * xs[dx] + c}, device_id_type=MESH_ID)

    c_hid.wait()
    nt = D // 128
    UN = 8

    def sum_step(i, a):
        for u in range(UN):
            a = a + hid_v[:, pl.ds(pl.multiple_of((i * UN + u) * 128, 128), 128)].astype(F32)
        return a

    tot = lax.fori_loop(0, nt // UN, sum_step, jnp.zeros((B, 128), F32))
    mean = jnp.sum(tot, axis=1, keepdims=True) / D

    def var_step(i, a):
        for u in range(UN):
            v = hid_v[:, pl.ds(pl.multiple_of((i * UN + u) * 128, 128), 128)].astype(F32) - mean
            a = a + v * v
        return a

    sq = lax.fori_loop(0, nt // UN, var_step, jnp.zeros((B, 128), F32))
    rstd = lax.rsqrt(jnp.sum(sq, axis=1, keepdims=True) / D + 1e-5)
    c_gain.wait()
    c_bias.wait()
    gb_f[0] = 1.0 + gb_raw[0].astype(F32)
    gb_f[1] = gb_raw[1].astype(F32)

    def norm_step(i, _):
        for u in range(UN):
            j = i * UN + u
            col = c * (nt // 2) + j
            v = hid_v[:, pl.ds(pl.multiple_of(col * 128, 128), 128)].astype(F32)
            v = (v - mean) * rstd * gb_f[0, pl.ds(col, 1), :] + gb_f[1, pl.ds(col, 1), :]
            h_v[:, pl.ds(pl.multiple_of(j * 128, 128), 128)] = v.astype(BF16)
        return 0

    lax.fori_loop(0, nt // 2 // UN, norm_step, 0)

    c_len.wait()
    row = lax.broadcasted_iota(jnp.int32, (BH, strip), 0)
    lane = lax.broadcasted_iota(jnp.int32, (BH, strip), 1)
    pos = jnp.zeros((BH, strip), F32)
    for r in range(BH):
        pos = jnp.where(row == r, len_s[c * BH + r].astype(F32), pos)
    hl = jnp.where(lane >= HD, lane - HD, lane)
    il = jnp.where(hl >= half, hl - half, hl)
    freq = jnp.exp(il.astype(F32) * (-2.0 / rot * 9.210340371976184))
    ang = jnp.where(hl < rot, pos * freq, 0.0)
    cos_t = jnp.cos(ang)
    sin_t = jnp.sin(ang)
    sin_lo = jnp.where(hl < half, -sin_t, 0.0)
    sin_hi = jnp.where(hl >= half, sin_t, 0.0)

    pl.semaphore_wait(barrier, XN * TN)

    def q_step(i, a):
        wq_copy(i).wait()
        return a + dot(h_v[:, pl.ds(pl.multiple_of(i * KC, KC), KC)], wq_v[i])

    NB = 4
    a = lax.fori_loop(0, NB, q_step, jnp.zeros((B, QW), F32))

    c_cache[0].wait()
    c_cache[1].wait()

    def widen(b, _):
        k_snd[b] = kc_v[(1 - c) * BH + b].astype(F32)
        v_snd[b] = vc_v[(1 - c) * BH + b].astype(F32)
        return 0

    lax.fori_loop(0, BH, widen, 0)
    xk = remote(k_snd, k_rcv, s_cx.at[0], r_cx.at[0], partner)
    xv = remote(v_snd, v_rcv, s_cx.at[1], r_cx.at[1], partner)
    xk.start()
    xv.start()

    qp[...] = lax.fori_loop(NB, NQ, q_step, a)
    xq = remote(qp.at[theirs, :], q_in, s_qd.at[0], r_qd.at[0], partner)
    xq.start()

    @pl.when(x < XN // 2)
    def _():
        c_wk.wait()

    @pl.when(x >= XN // 2)
    def _():
        c_wv.wait()

    xq.wait()
    qb = qp[mine, :] + q_in[...]
    for i in range(QW // strip):
        sl = slice(i * strip, (i + 1) * strip)
        q_all[x, :, sl] = rope(qb[:, sl], cos_t, sin_lo, sin_hi, half).astype(BF16).astype(F32)
    qg = []
    for d in range(1, XN):
        cp = remote(q_all.at[x], q_all.at[x], s_qg.at[d], r_qg.at[x], xpeer(d))
        cp.start()
        qg.append(cp)

    kvp[...] = dot(h_v[:, pl.ds(pl.multiple_of((x % (XN // 2)) * KVR, KVR), KVR)], wkv_v[...])
    xkd = remote(kvp.at[theirs, :], kv_in, s_kd.at[0], r_kd.at[0], partner)
    xkd.start()
    xkd.wait()
    kv_all[x] = kvp[mine, :] + kv_in[...]
    kg = []
    for d in range(1, XN):
        cp = remote(kv_all.at[x], kv_all.at[x], s_kg.at[d], r_kg.at[x], xpeer(d))
        cp.start()
        kg.append(cp)

    for d in range(XN):
        if d:
            remote(q_all.at[x], q_all.at[xs[d]], s_qg.at[d], r_qg.at[xs[d]], xpeer(d)).wait_recv()
    for blk in range(XN):
        for j in range(HB):
            h = blk * HB + j
            v = q_all[blk, :, j * HD:(j + 1) * HD]
            qh[0, h * BH:(h + 1) * BH, :] = v[:, 0:128]
            qh[1, h * BH:(h + 1) * BH, 0:HD - 128] = v[:, 128:HD]

    c_cache[2].wait()
    c_cache[3].wait()
    xk.wait()
    xv.wait()
    lane2 = lax.broadcasted_iota(jnp.int32, (G, 2 * SL), 1)
    p_here = jnp.where(lane2 < SL, s * SL + lane2, other * SL + lane2 - SL)
    for b in range(BH):
        for kv in range(KVN):
            rows = pl.ds(kv * G * BH + b, G, stride=BH)
            q = jnp.concatenate([qh[0, rows, :], qh[1, rows, :]], axis=1)[:, 0:HD].astype(BF16)
            s0 = dot(q, kc_v[c * BH + b, kv])
            s1 = dot(q, k_rcv[b, kv].astype(BF16))
            score[b, kv] = jnp.concatenate([s0, s1], axis=1)
    neg = -jnp.inf
    tail_lane = lax.broadcasted_iota(jnp.int32, (G, 128), 1)
    for b in range(BH):
        n = len_s[c * BH + b]
        for kv in range(KVN):
            sc = jnp.where(p_here < n, score[b, kv] * scale, neg)
            m = jnp.max(sc, axis=1, keepdims=True)
            ms = jnp.where(m == neg, 0.0, m)
            w = jnp.exp(sc - ms)
            l = jnp.sum(w, axis=1, keepdims=True)
            wb = w.astype(BF16)
            pv = dot_t(wb[:, 0:SL], vc_v[c * BH + b, kv]) + dot_t(wb[:, SL:], v_rcv[b, kv].astype(BF16))
            tail = jnp.concatenate([pv[:, 128:HD], jnp.zeros((G, 256 - HD), F32)], axis=1)
            tail = jnp.where(tail_lane == HD - 128, m, jnp.where(tail_lane == HD - 127, l, tail))
            rows = pl.ds(kv * G * BH + b, G, stride=BH)
            ob[0, rows, :] = pv[:, 0:128]
            ob[1, rows, :] = tail

    cr = []
    for d in range(1, XN):
        cp = remote(ob.at[:, pl.ds(pl.multiple_of(xs[d] * RB, RB), RB), :], o_in.at[x], s_cr.at[d], r_cr.at[x], xpeer(d))
        cp.start()
        cr.append(cp)

    for d in range(1, XN):
        remote(kv_all.at[x], kv_all.at[xs[d]], s_kg.at[d], r_kg.at[xs[d]], xpeer(d)).wait_recv()
    kn = kv_all[0]
    vn = kv_all[XN // 2]
    for i in range(1, XN // 2):
        kn = kn + kv_all[i]
        vn = vn + kv_all[XN // 2 + i]
    kn = rope(kn, cos_t, sin_lo, sin_hi, half).astype(BF16).astype(F32)
    vn = vn.astype(BF16).astype(F32)
    kvn[:, 0:strip] = kn
    kvn[:, strip:2 * strip] = vn
    kv_out[mine, :] = kvn[...]
    xe = remote(kvn, kv_out.at[mine, :], s_ke.at[0], r_ke.at[0], partner)
    xe.start()
    second = x >= XN // 2
    kh = jnp.where(second, kn[:, HD:], kn[:, 0:HD])
    vh = jnp.where(second, vn[:, HD:], vn[:, 0:HD])

    own = pl.ds(pl.multiple_of(x * RB, RB), RB)
    q_own = jnp.concatenate([qh[0, own, :], qh[1, own, :]], axis=1)[:, 0:HD]
    k_rep = jnp.concatenate([kh] * HB, axis=0)
    v_rep = jnp.concatenate([vh] * HB, axis=0)
    self_s = jnp.sum(q_own * k_rep, axis=1, keepdims=True) * scale
    for d in range(1, XN):
        remote(ob.at[:, own, :], o_in.at[xs[d]], s_cr.at[d], r_cr.at[xs[d]], xpeer(d)).wait_recv()
    o_in[x] = ob[:, own, :]
    parts = [jnp.concatenate([o_in[i, 0], o_in[i, 1]], axis=1) for i in range(XN)]
    ms = [p[:, HD:HD + 1] for p in parts]
    ls = [p[:, HD + 1:HD + 2] for p in parts]
    top = self_s
    for m in ms:
        top = jnp.maximum(top, m)
    f_self = jnp.exp(self_s - top)
    num = f_self * v_rep
    den = f_self
    for p, m, l in zip(parts, ms, ls):
        f = jnp.exp(m - top)
        num = num + f * p[:, 0:HD]
        den = den + f * l
    ctx = (num / den).astype(BF16).astype(F32)
    for j in range(HB):
        ctx_own[:, j * HD:(j + 1) * HD] = ctx[j * BH:(j + 1) * BH, :]

    cg = []
    cf = []
    ctx_in[x, mine, :] = ctx_own[...]
    cp = remote(ctx_own, ctx_in.at[x, mine, :], s_cf.at[0], r_cf.at[x], partner)
    cp.start()
    cf.append(cp)
    order = [1, XN - 1] + list(range(2, XN - 1))
    for d in order:
        cp = remote(ctx_own, ctx_in.at[x, mine, :], s_cg.at[d], r_cg.at[x], xpeer(d))
        cp.start()
        cg.append(cp)

    NW = 768
    for step, d in enumerate([0] + order):
        blk = xs[d]
        if d:
            remote(ctx_own, ctx_in.at[blk, mine, :], s_cg.at[d], r_cg.at[blk], xpeer(d)).wait_recv()
            cp = remote(ctx_in.at[blk, mine, :], ctx_in.at[blk, mine, :], s_cf.at[d], r_cf.at[blk], partner)
            cp.start()
            cf.append(cp)
        remote(ctx_own, ctx_in.at[blk, theirs, :], s_cf.at[d], r_cf.at[blk], partner).wait_recv()
        wo_copy(d).wait()
        lhs = ctx_in[blk].astype(BF16)
        for n in range(OW // NW):
            cs = slice(n * NW, (n + 1) * NW)
            r = dot(lhs, wo_v[d, :, cs])
            acc[:, cs] = r if step == 0 else acc[:, cs] + r

    def part(p):
        return (pl.ds(pl.multiple_of((p % 2) * BH, BH), BH), pl.ds(pl.multiple_of((p // 2) * PW, 128), PW))

    rsl = []
    for d in range(1, TN):
        rows, cols = part(ts[d])
        cp = remote(acc.at[rows, cols], rs_in.at[t], s_rs.at[d], r_rs.at[t], {'tp': ts[d]})
        cp.start()
        rsl.append(cp)
    rows, cols = part(t)
    for d in range(1, TN):
        remote(acc.at[rows, cols], rs_in.at[ts[d]], s_rs.at[d], r_rs.at[ts[d]], {'tp': ts[d]}).wait_recv()
    rs_in[t] = acc[rows, cols]
    tot = rs_in[0]
    for i in range(1, TN):
        tot = tot + rs_in[i]

    def place(sv, p):
        return out.at[pl.ds(pl.multiple_of((p % 2) * BH, BH), BH), pl.ds(pl.multiple_of(sv * OW + (p // 2) * PW, 128), PW)]

    place(s, t)[...] = tot
    og = []
    for dx in range(XN):
        for dt in range(TN):
            if dx or dt:
                cp = remote(place(s, t), place(s, t), s_og.at[dx * TN + dt], r_og.at[x * TN + t], {'tp': ts[dt], 'sp': 2 * xs[dx] + c})
                cp.start()
                og.append(cp)
    of = []
    for dx in range(XN):
        for dt in range(TN):
            src = place(2 * xs[dx] + c, ts[dt])
            if dx or dt:
                remote(src, src, s_og.at[dx * TN + dt], r_og.at[xs[dx] * TN + ts[dt]], partner).wait_recv()
            cp = remote(src, src, s_of.at[dx * TN + dt], r_of.at[xs[dx] * TN + ts[dt]], partner)
            cp.start()
            of.append(cp)
    for dx in range(XN):
        for dt in range(TN):
            src = place(2 * xs[dx] + 1 - c, ts[dt])
            remote(src, src, s_of.at[dx * TN + dt], r_of.at[xs[dx] * TN + ts[dt]], partner).wait_recv()
    xe_in = remote(kvn, kv_out.at[theirs, :], s_ke.at[0], r_ke.at[0], partner)
    xe_in.wait_recv()
    for cp in qg + kg + cr + [xe] + cg + cf + rsl + og + of:
        cp.wait_send()


def solution(mesh):
    TN = mesh.shape['tp']
    SN = mesh.shape['sp']
    XN = SN // 2

    def local_step(hidden, ln_gain, ln_bias, w_q, w_k, w_v, w_o, k_cache, v_cache, lengths):
        B, D = hidden.shape
        _, SL, KVN, HD = k_cache.shape
        G = w_q.shape[1] // (HD * KVN)
        BH = B // 2
        QW = w_q.shape[1] // XN
        KH = D // 2
        KC = 1024
        NQ = KH // KC
        KVR = KH // (XN // 2)
        HB = QW // HD
        OW = D // SN
        PW = OW // 2
        KW = KVN * HD
        assert w_k.shape[1] == KW and KH % KC == 0 and TN == 4 and XN % 2 == 0 and KVN == 2
        k_t = jnp.transpose(k_cache, (0, 2, 3, 1))
        v_t = jnp.transpose(v_cache, (0, 2, 3, 1))
        gain = ln_gain.reshape(D // 128, 128)
        bias = ln_bias.reshape(D // 128, 128)
        V = pltpu.VMEM
        dma = pltpu.SemaphoreType.DMA
        scratch = [
            V((B, D), BF16), V((2, D // 128, 128), BF16), V((2, D // 128, 128), F32), V((B, KH), BF16), pltpu.SMEM((B,), jnp.int32),
            V((NQ, KC, QW), BF16), V((KVR, KW), BF16), V((XN, QW, OW), BF16),
            V((B, KVN, HD, SL), BF16), V((B, KVN, HD, SL), BF16),
            V((BH, KVN, HD, SL), F32), V((BH, KVN, HD, SL), F32), V((BH, KVN, HD, SL), F32), V((BH, KVN, HD, SL), F32),
            V((B, QW), F32), V((BH, QW), F32), V((XN, BH, QW), F32), V((2, XN * HB * BH, 128), F32),
            V((B, KW), F32), V((BH, KW), F32), V((XN, BH, KW), F32), V((BH, 2 * KW), F32),
            V((BH, KVN, G, 2 * SL), F32), V((2, XN * HB * BH, 128), F32), V((XN, 2, HB * BH, 128), F32),
            V((BH, QW), F32), V((XN, B, QW), F32), V((B, OW), F32), V((TN, BH, PW), F32),
            dma((4,)), dma((4,)), dma((NQ,)), dma((1,)), dma((XN,)),
            dma((2,)), dma((2,)), dma((1,)), dma((1,)), dma((XN,)), dma((XN,)), dma((1,)), dma((1,)), dma((XN,)), dma((XN,)), dma((1,)), dma((1,)),
            dma((XN,)), dma((XN,)), dma((XN,)), dma((XN,)), dma((XN,)), dma((XN,)), dma((TN,)), dma((TN,)),
            dma((XN * TN,)), dma((XN * TN,)), dma((XN * TN,)), dma((XN * TN,)),
        ]
        cfg = (XN, TN, HD, G, KC, HD ** -0.5)
        summed, kv_new = pl.pallas_call(
            functools.partial(kernel, cfg),
            out_shape=(jax.ShapeDtypeStruct((B, D), F32), jax.ShapeDtypeStruct((B, 2 * KW), F32)),
            in_specs=[pl.BlockSpec(memory_space=pl.ANY)] * 10,
            out_specs=(pl.BlockSpec(memory_space=pltpu.VMEM), pl.BlockSpec(memory_space=pltpu.VMEM)),
            scratch_shapes=scratch,
            compiler_params=pltpu.CompilerParams(collective_id=0, has_side_effects=True, vmem_limit_bytes=67043328),
            name='decode_step',
        )(hidden, gain, bias, w_q, w_k, w_v, w_o, k_t, v_t, lengths)
        out = (hidden.astype(F32) + summed).astype(BF16)
        k_new = kv_new[:, :KW].astype(BF16).reshape(B, KVN, HD)
        v_new = kv_new[:, KW:].astype(BF16).reshape(B, KVN, HD)
        return out, k_new, v_new

    row_spec = P('dp', None)
    cache_spec = P('dp', 'sp', 'tp', None)
    head_spec = P('dp', 'tp', None)
    return jax.shard_map(local_step, mesh=mesh, in_specs=(row_spec, P(None), P(None), P(None, 'tp'), P(None, 'tp'), P(None, 'tp'), P('tp', None), cache_spec, cache_spec, P('dp')), out_specs=(row_spec, head_spec, head_spec), check_vma=False)
```

time: 224 us -> 64 us (0.29)
  matrix products: 122 us -> 0 us
  waiting for transfers between devices: 68.1 us -> 0 us
  Pallas kernels: 0 us -> 58.7 us
  between operations: 14.3 us -> 0.64 us
  other arithmetic: 12.7 us -> 3.14 us
  local copies, waits for them, and re-layouts: 5.46 us -> 1.4 us
    dot_general x7 -> x0, matrix products: 122 us -> none  [the longest x1 53.5 us: local_step(): partial_out = jnp.dot(context, w_o, preferred_element_type=jnp.float32)]
    pallas_call x0 -> x1, Pallas kernels: none -> 58.7 us  [local_step(): pl.pallas_call(functools.partial(kernel, cfg), out_shape=(jax.ShapeDtypeS...]
    psum x1 -> x0, waiting for transfers between devices: 38.9 us -> none  [local_step(): summed = lax.psum(partial_out, 'tp')]
    all_gather x1 -> x0, waiting for transfers between devices: 29.1 us -> none  [local_step(): gathered = lax.all_gather(packed, 'sp', axis=0)]
    reduce_sum x5 -> x0, other arithmetic: 3.53 us -> none  [the longest x1 1.4 us: norm_one_plus(): row_var = jnp.mean(centred * centred, axis=-1, keepdims=True)]
    all_gather x1 -> x0, local copies, waits for them, and re-layouts: 2.9 us -> none  [local_step(): gathered = lax.all_gather(packed, 'sp', axis=0)]
  transfers between devices with their start and end apart: 2 -> 0, of which waited for: 2 -> 0; matrix products, arithmetic and copies ran while one was open for 0% -> 0% of each run, Pallas kernels for 0% -> 0%
where the time goes in v1:
time: 64 us; the launch traced here: 63.8 us
  Pallas kernels  58.7 us (92%)
  other arithmetic  3.14 us (5%)
  local copies, waits for them, and re-layouts  1.4 us (2%)
  between operations  0.64 us (1%)
    pallas_call x1, Pallas kernels, local_step(): pl.pallas_call(functools.partial(kernel, cfg), out_shape=(jax.ShapeDtypeS...  58.7 us
    convert_element_type x1, other arithmetic, local_step(): out = (hidden.astype(F32) + summed).astype(BF16)  2.33 us

profile of v1, /device:TPU:97, one launch (start us, length us, event | category | flops | bytes accessed | tf_op | source)
XLA Modules:
  0.0 63.8 jit_solution(15026308530526963243)
XLA Ops:
  0.6 58.7 %decode_step.1 = (f32[16,18432]{1,0:T(8,128)}, f32[16,768]{1,0:T(8,128)}) custom-call(bf16[16,18432]{1,0:T(8,128)(2,1)} %hidden.1, bf16[144,128]{1,0:T(8,128)(2,1)} %bitcast.6, bf16[144,128]{1,0:T(8,128)(2,1)} %bitcast.7, bf16[18432,4608]{1,0:T(8,128)(2,1)} %w_q.1, bf16[18432,384]{1,0:T(8,128)(2,1)} %w_k.1, bf16[18432,384]{1,0:T(8,128)(2,1)} %w_v.1, ...), custom_call_target="tpu_custom_call" | custom-call | tf_op jit(solution)/shard_map/decode_step/pallas_call | solution.py:435
  59.3 0.8 %convert.4 = bf16[16,768]{1,0:T(8,128)(2,1)S(1)} convert(f32[16,768]{1,0:T(8,128)} %get-tuple-element.6) | non-fusion elementwise | flops 12288 | bytes 73728 | tf_op jit(solution)/shard_map/convert.1
  60.1 0.7 %reshape.20 = bf16[16,2,192]{2,1,0:T(2,128)(2,1)} reshape(bf16[16,384]{1,0:T(8,128)(2,1)S(1)} %get-tuple-element.8) | data formatting | bytes 24576 | tf_op jit(solution)/shard_map/reshape | solution.py:445
  60.8 0.7 %reshape.21 = bf16[16,2,192]{2,1,0:T(2,128)(2,1)} reshape(bf16[16,384]{1,0:T(8,128)(2,1)S(1)} %get-tuple-element.7) | data formatting | bytes 24576 | tf_op jit(solution)/shard_map/reshape | solution.py:446
  61.5 2.3 %add_convert_fusion = bf16[16,18432]{1,0:T(8,128)(2,1)} fusion(f32[16,18432]{1,0:T(8,128)} %get-tuple-element.5, bf16[16,18432]{1,0:T(8,128)(2,1)} %hidden.1), kind=kLoop, calls=%fused_computation | loop fusion | flops 884736 | bytes 2359296 | tf_op jit(solution)/shard_map/convert_element_type | solution.py:444
  (1 shorter events, 0.0 us)

commit v2 on v1

--- a/solution.py
+++ b/solution.py
@@ -27,12 +27,12 @@
     return u * cos_t + ahead * sin_lo + behind * sin_hi
 
 
-def kernel(cfg, hidden, gain, bias, w_q, w_k, w_v, w_o, k_t, v_t, lens, out, kv_out,
+def kernel(cfg, hidden, gain, bias, w_q, w_k, w_v, w_o, k_t, v_t, lens, out, k_out, v_out,
            hid_v, gb_raw, gb_f, h_v, len_s, wq_v, wkv_v, wo_v, kc_v, vc_v, k_snd, v_snd, k_rcv, v_rcv,
-           qp, q_in, q_all, qh, kvp, kv_in, kv_all, kvn, score, ob, o_in, ctx_own, ctx_in, acc, rs_in,
-           sem_small, sem_cache, sem_wq, sem_wkv, sem_wo,
+           og_v, ob_v, kv_rcv, qp, q_in, q_all, qh, kvp, kv_in, kv_all, kvn, score, ob, o_in, ctx_own, ctx_all, part, p1_in, p2_in,
+           sem_small, sem_cache, sem_wq, sem_wkv, sem_wo, sem_out,
            s_cx, r_cx, s_qd, r_qd, s_qg, r_qg, s_kd, r_kd, s_kg, r_kg, s_ke, r_ke,
-           s_cr, r_cr, s_cg, r_cg, s_cf, r_cf, s_rs, r_rs, s_og, r_og, s_of, r_of):
+           s_cr, r_cr, s_cf, r_cf, s_p1, r_p1, s_p2, r_p2, s_ag, r_ag, s_of, r_of):
     XN, TN, HD, G, KC, scale = cfg
     B, D = hidden.shape
     BH = B // 2
@@ -44,6 +44,7 @@
     HB = QW // HD
     OW = D // (2 * XN)
     PW = OW // 2
+    NP = 4
     rot = HD // 2
     half = rot // 2
     strip = 2 * HD
@@ -83,33 +84,48 @@
     def wq_copy(i):
         return pltpu.make_async_copy(w_q.at[pl.ds(pl.multiple_of(c * KH + i * KC, KC), KC), qcol], wq_v.at[i], sem_wq.at[i])
 
-    for i in range(2):
-        wq_copy(i).start()
     c_cache[0].start()
     c_cache[1].start()
-    for i in range(2, NQ):
-        wq_copy(i).start()
-    c_cache[2].start()
-    c_cache[3].start()
+    wq_copy(0).start()
+    wq_copy(1).start()
     kvrow = pl.ds(pl.multiple_of(c * KH + (x % (XN // 2)) * KVR, KVR), KVR)
     c_wk = pltpu.make_async_copy(w_k.at[kvrow, :], wkv_v, sem_wkv.at[0])
     c_wv = pltpu.make_async_copy(w_v.at[kvrow, :], wkv_v, sem_wkv.at[0])
 
-    @pl.when(x < XN // 2)
-    def _():
-        c_wk.start()
-
-    @pl.when(x >= XN // 2)
-    def _():
-        c_wv.start()
-
-    ocol = pl.ds(pl.multiple_of(s * OW, 128), OW)
+    def start_wkv():
+        @pl.when(x < XN // 2)
+        def _():
+            c_wk.start()
+
+        @pl.when(x >= XN // 2)
+        def _():
+            c_wv.start()
+
+    k1 = x * (1 - c) + t * c
+    k2 = x * c + t * (1 - c)
+    k1s = [(k1 + d) % XN for d in range(XN)]
+    k2s = [(k2 + d) % XN for d in range(XN)]
+
+    def along1(d):
+        return {'tp': (t + c * d) % TN, 'sp': 2 * ((x + (1 - c) * d) % XN) + c}
+
+    def along2(d):
+        return {'tp': (t + (1 - c) * d) % TN, 'sp': 2 * ((x + c * d) % XN) + c}
 
     def wo_copy(d):
-        return pltpu.make_async_copy(w_o.at[pl.ds(pl.multiple_of(xs[d] * QW, QW), QW), ocol], wo_v.at[d], sem_wo.at[d])
-
-    for d in (0, 1, XN - 1) + tuple(range(2, XN - 1)):
-        wo_copy(d).start()
+        cols = pl.ds(pl.multiple_of(c * (D // 2) + k1s[d] * OW, 128), OW)
+        return pltpu.make_async_copy(w_o.at[pl.ds(pl.multiple_of(x * QW, QW), QW), cols], wo_v.at[d], sem_wo.at[d])
+
+    order = [1, XN - 1] + list(range(2, XN - 1))
+    later = [functools.partial(lambda i: wq_copy(i).start(), i) for i in range(2, NQ)]
+    later += [start_wkv, c_cache[2].start, c_cache[3].start]
+    far_first = [2, 1, 3, 0]
+    later += [functools.partial(lambda d: wo_copy(d).start(), d) for d in far_first]
+
+    def issue(n):
+        for _ in range(n):
+            if later:
+                later.pop(0)()
 
     barrier = pltpu.get_barrier_semaphore()
     pl.semaphore_signal(barrier, inc=1, device_id=partner, device_id_type=MESH_ID)
@@ -137,9 +153,11 @@
         return a
 
     sq = lax.fori_loop(0, nt // UN, var_step, jnp.zeros((B, 128), F32))
+    issue(1)
     rstd = lax.rsqrt(jnp.sum(sq, axis=1, keepdims=True) / D + 1e-5)
     c_gain.wait()
     c_bias.wait()
+    issue(1)
     gb_f[0] = 1.0 + gb_raw[0].astype(F32)
     gb_f[1] = gb_raw[1].astype(F32)
 
@@ -171,13 +189,6 @@
 
     pl.semaphore_wait(barrier, XN * TN)
 
-    def q_step(i, a):
-        wq_copy(i).wait()
-        return a + dot(h_v[:, pl.ds(pl.multiple_of(i * KC, KC), KC)], wq_v[i])
-
-    NB = 4
-    a = lax.fori_loop(0, NB, q_step, jnp.zeros((B, QW), F32))
-
     c_cache[0].wait()
     c_cache[1].wait()
 
@@ -192,17 +203,16 @@
     xk.start()
     xv.start()
 
-    qp[...] = lax.fori_loop(NB, NQ, q_step, a)
+    a = None
+    for i in range(NQ):
+        wq_copy(i).wait()
+        issue(1)
+        r = dot(h_v[:, i * KC:(i + 1) * KC], wq_v[i])
+        a = r if a is None else a + r
+    issue(len(later))
+    qp[...] = a
     xq = remote(qp.at[theirs, :], q_in, s_qd.at[0], r_qd.at[0], partner)
     xq.start()
-
-    @pl.when(x < XN // 2)
-    def _():
-        c_wk.wait()
-
-    @pl.when(x >= XN // 2)
-    def _():
-        c_wv.wait()
 
     xq.wait()
     qb = qp[mine, :] + q_in[...]
@@ -214,6 +224,14 @@
         cp = remote(q_all.at[x], q_all.at[x], s_qg.at[d], r_qg.at[x], xpeer(d))
         cp.start()
         qg.append(cp)
+
+    @pl.when(x < XN // 2)
+    def _():
+        c_wk.wait()
+
+    @pl.when(x >= XN // 2)
+    def _():
+        c_wv.wait()
 
     kvp[...] = dot(h_v[:, pl.ds(pl.multiple_of((x % (XN // 2)) * KVR, KVR), KVR)], wkv_v[...])
     xkd = remote(kvp.at[theirs, :], kv_in, s_kd.at[0], r_kd.at[0], partner)
@@ -284,8 +302,8 @@
     vn = vn.astype(BF16).astype(F32)
     kvn[:, 0:strip] = kn
     kvn[:, strip:2 * strip] = vn
-    kv_out[mine, :] = kvn[...]
-    xe = remote(kvn, kv_out.at[mine, :], s_ke.at[0], r_ke.at[0], partner)
+    kv_rcv[mine, :] = kvn[...]
+    xe = remote(kvn, kv_rcv.at[mine, :], s_ke.at[0], r_ke.at[0], partner)
     xe.start()
     second = x >= XN // 2
     kh = jnp.where(second, kn[:, HD:], kn[:, 0:HD])
@@ -316,79 +334,102 @@
     for j in range(HB):
         ctx_own[:, j * HD:(j + 1) * HD] = ctx[j * BH:(j + 1) * BH, :]
 
-    cg = []
-    cf = []
-    ctx_in[x, mine, :] = ctx_own[...]
-    cp = remote(ctx_own, ctx_in.at[x, mine, :], s_cf.at[0], r_cf.at[x], partner)
-    cp.start()
-    cf.append(cp)
-    order = [1, XN - 1] + list(range(2, XN - 1))
-    for d in order:
-        cp = remote(ctx_own, ctx_in.at[x, mine, :], s_cg.at[d], r_cg.at[x], xpeer(d))
-        cp.start()
-        cg.append(cp)
-
-    NW = 768
-    for step, d in enumerate([0] + order):
-        blk = xs[d]
-        if d:
-            remote(ctx_own, ctx_in.at[blk, mine, :], s_cg.at[d], r_cg.at[blk], xpeer(d)).wait_recv()
-            cp = remote(ctx_in.at[blk, mine, :], ctx_in.at[blk, mine, :], s_cf.at[d], r_cf.at[blk], partner)
-            cp.start()
-            cf.append(cp)
-        remote(ctx_own, ctx_in.at[blk, theirs, :], s_cf.at[d], r_cf.at[blk], partner).wait_recv()
+    ctx_all[mine, :] = ctx_own[...]
+    cf = remote(ctx_own, ctx_all.at[mine, :], s_cf.at[0], r_cf.at[0], partner)
+    cf.start()
+    remote(ctx_own, ctx_all.at[theirs, :], s_cf.at[0], r_cf.at[0], partner).wait_recv()
+
+    lhs = ctx_all[...].astype(BF16)
+    sends = [xe, cf]
+
+    def send(src, dst, ss, rs, dev):
+        cp = remote(src, dst, ss, rs, dev)
+        cp.start()
+        sends.append(cp)
+
+    for d in far_first:
         wo_copy(d).wait()
-        lhs = ctx_in[blk].astype(BF16)
-        for n in range(OW // NW):
-            cs = slice(n * NW, (n + 1) * NW)
-            r = dot(lhs, wo_v[d, :, cs])
-            acc[:, cs] = r if step == 0 else acc[:, cs] + r
-
-    def part(p):
-        return (pl.ds(pl.multiple_of((p % 2) * BH, BH), BH), pl.ds(pl.multiple_of((p // 2) * PW, 128), PW))
-
-    rsl = []
-    for d in range(1, TN):
-        rows, cols = part(ts[d])
-        cp = remote(acc.at[rows, cols], rs_in.at[t], s_rs.at[d], r_rs.at[t], {'tp': ts[d]})
-        cp.start()
-        rsl.append(cp)
-    rows, cols = part(t)
-    for d in range(1, TN):
-        remote(acc.at[rows, cols], rs_in.at[ts[d]], s_rs.at[d], r_rs.at[ts[d]], {'tp': ts[d]}).wait_recv()
-    rs_in[t] = acc[rows, cols]
-    tot = rs_in[0]
-    for i in range(1, TN):
-        tot = tot + rs_in[i]
-
-    def place(sv, p):
-        return out.at[pl.ds(pl.multiple_of((p % 2) * BH, BH), BH), pl.ds(pl.multiple_of(sv * OW + (p // 2) * PW, 128), PW)]
-
-    place(s, t)[...] = tot
-    og = []
-    for dx in range(XN):
-        for dt in range(TN):
-            if dx or dt:
-                cp = remote(place(s, t), place(s, t), s_og.at[dx * TN + dt], r_og.at[x * TN + t], {'tp': ts[dt], 'sp': 2 * xs[dx] + c})
-                cp.start()
-                og.append(cp)
-    of = []
-    for dx in range(XN):
-        for dt in range(TN):
-            src = place(2 * xs[dx] + c, ts[dt])
-            if dx or dt:
-                remote(src, src, s_og.at[dx * TN + dt], r_og.at[xs[dx] * TN + ts[dt]], partner).wait_recv()
-            cp = remote(src, src, s_of.at[dx * TN + dt], r_of.at[xs[dx] * TN + ts[dt]], partner)
-            cp.start()
-            of.append(cp)
-    for dx in range(XN):
-        for dt in range(TN):
-            src = place(2 * xs[dx] + 1 - c, ts[dt])
-            remote(src, src, s_of.at[dx * TN + dt], r_of.at[xs[dx] * TN + ts[dt]], partner).wait_recv()
-    xe_in = remote(kvn, kv_out.at[theirs, :], s_ke.at[0], r_ke.at[0], partner)
+    for h in range(2):
+        for d in far_first:
+            r = dot(lhs, wo_v[d, :, h * PW:(h + 1) * PW])
+            part[d, 2 * h] = r[0:BH]
+            part[d, 2 * h + 1] = r[BH:]
+            if d:
+                for p in (2 * h, 2 * h + 1):
+                    send(part.at[d, p], p1_in.at[k1, p], s_p1.at[d * NP + p], r_p1.at[k1 * NP + p], along1(d))
+
+    for p in range(NP):
+        for d in range(1, XN):
+            remote(part.at[d, p], p1_in.at[k1s[d], p], s_p1.at[d * NP + p], r_p1.at[k1s[d] * NP + p], partner).wait_recv()
+        p2_in[k2, p] = part[0, p] + p1_in[k1s[1], p] + p1_in[k1s[2], p] + p1_in[k1s[3], p]
+        for d in order:
+            send(p2_in.at[k2, p], p2_in.at[k2, p], s_p2.at[d * NP + p], r_p2.at[k2 * NP + p], along2(d))
+
+    def place(k, p, cc):
+        return (p % 2) * BH, pl.multiple_of(cc * (D // 2) + k * OW + (p // 2) * PW, 128)
+
+    def view(k, p, cc):
+        r0, c0 = place(k, p, cc)
+        return og_v.at[r0:r0 + BH, pl.ds(c0, PW)]
+
+    stores = []
+
+    def store(i, k, p, cc):
+        r0, c0 = place(k, p, cc)
+        ob_v[i] = og_v[r0:r0 + BH, pl.ds(c0, PW)].astype(BF16)
+        cp = pltpu.make_async_copy(ob_v.at[i], out.at[r0:r0 + BH, pl.ds(c0, PW)], sem_out.at[i])
+        cp.start()
+        stores.append(cp)
+
+    for p in range(NP):
+        for d in range(1, XN):
+            remote(part.at[d, p], p2_in.at[k2s[d], p], s_p2.at[d * NP + p], r_p2.at[k2s[d] * NP + p], partner).wait_recv()
+        r0, c0 = place(k1, p, c)
+        tot = p2_in[0, p] + p2_in[1, p] + p2_in[2, p] + p2_in[3, p]
+        res = hid_v[:, pl.ds(c0, PW)].astype(F32)[r0:r0 + BH]
+        og_v[r0:r0 + BH, pl.ds(c0, PW)] = (res + tot).astype(BF16).astype(F32)
+        mine_p = view(k1, p, c)
+        for d in order:
+            send(mine_p, mine_p, s_ag.at[d * NP + p], r_ag.at[k1 * NP + p], along1(d))
+        send(mine_p, mine_p, s_of.at[p], r_of.at[k1 * NP + p], partner)
+    for p in range(NP):
+        store(p, k1, p, c)
+    for p in range(NP):
+        for d in order:
+            ref = view(k1s[d], p, c)
+            remote(ref, ref, s_ag.at[d * NP + p], r_ag.at[k1s[d] * NP + p], partner).wait_recv()
+            send(ref, ref, s_of.at[d * NP + p], r_of.at[k1s[d] * NP + p], partner)
+            store(d * NP + p, k1s[d], p, c)
+    for d in [0] + order:
+        for p in range(NP):
+            ref = view(k2s[d], p, 1 - c)
+            remote(ref, ref, s_of.at[d * NP + p], r_of.at[k2s[d] * NP + p], partner).wait_recv()
+            store(XN * NP + d * NP + p, k2s[d], p, 1 - c)
+    xe_in = remote(kvn, kv_rcv.at[theirs, :], s_ke.at[0], r_ke.at[0], partner)
     xe_in.wait_recv()
-    for cp in qg + kg + cr + [xe] + cg + cf + rsl + og + of:
+    k_out[...] = kv_rcv[:, 0:strip]
+    v_out[...] = kv_rcv[:, strip:2 * strip]
+    for cp in qg + kg + cr + sends:
         cp.wait_send()
+    for cp in stores:
+        cp.wait()
+
+
+def hand_on(o_in, k_in, v_in, o_out, k_out, v_out, buf, s_in, s_out):
+    n, _, w = buf.shape
+    reads = [pltpu.make_async_copy(o_in.at[:, i * w:(i + 1) * w], buf.at[i], s_in.at[i]) for i in range(n)]
+    writes = [pltpu.make_async_copy(buf.at[i], o_out.at[:, i * w:(i + 1) * w], s_out.at[i]) for i in range(n)]
+    for r in reads:
+        r.start()
+    hd = k_out.shape[2]
+    for j in range(k_out.shape[1]):
+        k_out[:, j, :] = k_in[:, j * hd:(j + 1) * hd].astype(BF16)
+        v_out[:, j, :] = v_in[:, j * hd:(j + 1) * hd].astype(BF16)
+    for r, w in zip(reads, writes):
+        r.wait()
+        w.start()
+    for w in writes:
+        w.wait()
 
 
 def solution(mesh):
@@ -410,7 +451,7 @@
         OW = D // SN
         PW = OW // 2
         KW = KVN * HD
-        assert w_k.shape[1] == KW and KH % KC == 0 and TN == 4 and XN % 2 == 0 and KVN == 2
+        assert w_k.shape[1] == KW and KH % KC == 0 and XN == TN == 4 and KVN == 2
         k_t = jnp.transpose(k_cache, (0, 2, 3, 1))
         v_t = jnp.transpose(v_cache, (0, 2, 3, 1))
         gain = ln_gain.reshape(D // 128, 128)
@@ -422,29 +463,32 @@
             V((NQ, KC, QW), BF16), V((KVR, KW), BF16), V((XN, QW, OW), BF16),
             V((B, KVN, HD, SL), BF16), V((B, KVN, HD, SL), BF16),
             V((BH, KVN, HD, SL), F32), V((BH, KVN, HD, SL), F32), V((BH, KVN, HD, SL), F32), V((BH, KVN, HD, SL), F32),
+            V((B, D), F32), V((2 * XN * 4, BH, PW), BF16), V((B, 2 * KW), F32),
             V((B, QW), F32), V((BH, QW), F32), V((XN, BH, QW), F32), V((2, XN * HB * BH, 128), F32),
             V((B, KW), F32), V((BH, KW), F32), V((XN, BH, KW), F32), V((BH, 2 * KW), F32),
             V((BH, KVN, G, 2 * SL), F32), V((2, XN * HB * BH, 128), F32), V((XN, 2, HB * BH, 128), F32),
-            V((BH, QW), F32), V((XN, B, QW), F32), V((B, OW), F32), V((TN, BH, PW), F32),
-            dma((4,)), dma((4,)), dma((NQ,)), dma((1,)), dma((XN,)),
+            V((BH, QW), F32), V((B, QW), F32), V((XN, 4, BH, PW), F32), V((XN, 4, BH, PW), F32), V((XN, 4, BH, PW), F32),
+            dma((4,)), dma((4,)), dma((NQ,)), dma((1,)), dma((XN,)), dma((2 * XN * 4,)),
             dma((2,)), dma((2,)), dma((1,)), dma((1,)), dma((XN,)), dma((XN,)), dma((1,)), dma((1,)), dma((XN,)), dma((XN,)), dma((1,)), dma((1,)),
-            dma((XN,)), dma((XN,)), dma((XN,)), dma((XN,)), dma((XN,)), dma((XN,)), dma((TN,)), dma((TN,)),
-            dma((XN * TN,)), dma((XN * TN,)), dma((XN * TN,)), dma((XN * TN,)),
+            dma((XN,)), dma((XN,)), dma((1,)), dma((1,)), dma((XN * 4,)), dma((XN * 4,)), dma((XN * 4,)), dma((XN * 4,)),
+            dma((XN * 4,)), dma((XN * 4,)), dma((XN * 4,)), dma((XN * 4,)),
         ]
         cfg = (XN, TN, HD, G, KC, HD ** -0.5)
-        summed, kv_new = pl.pallas_call(
+        out, k_new, v_new = pl.pallas_call(
             functools.partial(kernel, cfg),
-            out_shape=(jax.ShapeDtypeStruct((B, D), F32), jax.ShapeDtypeStruct((B, 2 * KW), F32)),
+            out_shape=(jax.ShapeDtypeStruct((B, D), BF16), jax.ShapeDtypeStruct((B, KW), F32), jax.ShapeDtypeStruct((B, KW), F32)),
             in_specs=[pl.BlockSpec(memory_space=pl.ANY)] * 10,
-            out_specs=(pl.BlockSpec(memory_space=pltpu.VMEM), pl.BlockSpec(memory_space=pltpu.VMEM)),
+            out_specs=(pl.BlockSpec(memory_space=pl.ANY),) + (pl.BlockSpec(memory_space=pltpu.VMEM),) * 2,
             scratch_shapes=scratch,
             compiler_params=pltpu.CompilerParams(collective_id=0, has_side_effects=True, vmem_limit_bytes=67043328),
             name='decode_step',
         )(hidden, gain, bias, w_q, w_k, w_v, w_o, k_t, v_t, lengths)
-        out = (hidden.astype(F32) + summed).astype(BF16)
-        k_new = kv_new[:, :KW].astype(BF16).reshape(B, KVN, HD)
-        v_new = kv_new[:, KW:].astype(BF16).reshape(B, KVN, HD)
-        return out, k_new, v_new
+        vm = pl.BlockSpec(memory_space=pltpu.VMEM)
+        hb = pl.BlockSpec(memory_space=pl.ANY)
+        head = jax.ShapeDtypeStruct((B, KVN, HD), BF16)
+        return pl.pallas_call(
+            hand_on, out_shape=(jax.ShapeDtypeStruct((B, D), BF16), head, head), in_specs=[hb, vm, vm], out_specs=(hb, vm, vm),
+            scratch_shapes=[V((4, B, D // 4), BF16), dma((4,)), dma((4,))], name='hand_on')(out, k_new, v_new)
 
     row_spec = P('dp', None)
     cache_spec = P('dp', 'sp', 'tp', None)

time: 64 us -> 49.9 us (0.78)
  Pallas kernels: 58.7 us -> 49.1 us
  other arithmetic: 3.14 us -> 0 us
  local copies, waits for them, and re-layouts: 1.4 us -> 0 us
    pallas_call x1, Pallas kernels: 58.7 us -> 45.8 us  [local_step(): pl.pallas_call(functools.partial(kernel, cfg), out_shape=(jax.ShapeDtypeS...]
    pallas_call x0 -> x1, Pallas kernels: none -> 3.22 us  [local_step(): pl.pallas_call(hand_on, out_shape=(jax.ShapeDtypeStruct((B, D), BF16), he...]
    convert_element_type x1 -> x0, other arithmetic: 2.33 us -> none  [local_step(): out = (hidden.astype(F32) + summed).astype(BF16)]
    reshape x2 -> x0, local copies, waits for them, and re-layouts: 1.39 us -> none  [the longest x1 0.7 us: local_step(): k_new = kv_new[:, :KW].astype(BF16).reshape(B, KVN, HD)]
    another operation x1 -> x0, other arithmetic: 0.8 us -> none
where the time goes in v2:
time: 49.9 us; the launch traced here: 49.7 us
  Pallas kernels  49.1 us (98%)
  between operations  0.64 us (1%)
    pallas_call x1, Pallas kernels, local_step(): pl.pallas_call(functools.partial(kernel, cfg), out_shape=(jax.ShapeDtypeS...  45.8 us
    pallas_call x1, Pallas kernels, local_step(): pl.pallas_call(hand_on, out_shape=(jax.ShapeDtypeStruct((B, D), BF16), he...  3.22 us

profile of v2, /device:TPU:97, one launch (start us, length us, event | category | flops | bytes accessed | tf_op | source)
XLA Modules:
  0.0 49.7 jit_solution(4543210016411706705)
XLA Ops:
  0.6 45.8 %decode_step.1 = (bf16[16,18432]{1,0:T(8,128)(2,1)}, f32[16,384]{1,0:T(8,128)}, f32[16,384]{1,0:T(8,128)}) custom-call(bf16[16,18432]{1,0:T(8,128)(2,1)} %hidden.1, bf16[144,128]{1,0:T(8,128)(2,1)} %bitcast.6, bf16[144,128]{1,0:T(8,128)(2,1)} %bitcast.7, bf16[18432,4608]{1,0:T(8,128)(2,1)} %w_q.1, bf16[18432,384]{1,0:T(8,128)(2,1)} %w_k.1, ...), custom_call_target="tpu_custom_call" | custom-call | tf_op jit(solution)/shard_map/decode_step/pallas_call | solution.py:477
  46.5 3.2 %hand_on.1 = (bf16[16,18432]{1,0:T(8,128)(2,1)}, bf16[16,2,192]{2,1,0:T(2,128)(2,1)}, bf16[16,2,192]{2,1,0:T(2,128)(2,1)}) custom-call(bf16[16,18432]{1,0:T(8,128)(2,1)} %get-tuple-element.6.o_in, f32[16,384]{1,0:T(8,128)} %get-tuple-element.7.k_in, f32[16,384]{1,0:T(8,128)} %get-tuple-element.8.v_in), custom_call_target="tpu_custom_call" | custom-call | tf_op jit(solution)/shard_map/hand_on/pallas_call | solution.py:489

commit v3 on v2

--- a/solution.py
+++ b/solution.py
@@ -43,8 +43,9 @@
     KVR = KH // (XN // 2)
     HB = QW // HD
     OW = D // (2 * XN)
-    PW = OW // 2
-    NP = 4
+    NH = 3
+    PW = OW // NH
+    NP = 2 * NH
     rot = HD // 2
     half = rot // 2
     strip = 2 * HD
@@ -101,26 +102,25 @@
         def _():
             c_wv.start()
 
-    k1 = x * (1 - c) + t * c
-    k2 = x * c + t * (1 - c)
-    k1s = [(k1 + d) % XN for d in range(XN)]
-    k2s = [(k2 + d) % XN for d in range(XN)]
-
-    def along1(d):
-        return {'tp': (t + c * d) % TN, 'sp': 2 * ((x + (1 - c) * d) % XN) + c}
-
-    def along2(d):
-        return {'tp': (t + (1 - c) * d) % TN, 'sp': 2 * ((x + c * d) % XN) + c}
-
-    def wo_copy(d):
-        cols = pl.ds(pl.multiple_of(c * (D // 2) + k1s[d] * OW, 128), OW)
-        return pltpu.make_async_copy(w_o.at[pl.ds(pl.multiple_of(x * QW, QW), QW), cols], wo_v.at[d], sem_wo.at[d])
+    axis = [(c + h) % 2 for h in range(NH)]
+    k1 = [x * (1 - a) + t * a for a in axis]
+    k2 = [x * a + t * (1 - a) for a in axis]
+
+    def along1(h, d):
+        return {'tp': (t + axis[h] * d) % TN, 'sp': 2 * ((x + (1 - axis[h]) * d) % XN) + c}
+
+    def along2(h, d):
+        return {'tp': (t + (1 - axis[h]) * d) % TN, 'sp': 2 * ((x + axis[h] * d) % XN) + c}
+
+    def wo_copy(h, d):
+        cols = pl.ds(pl.multiple_of(c * (D // 2) + (k1[h] + d) % XN * OW + h * PW, 128), PW)
+        return pltpu.make_async_copy(w_o.at[pl.ds(pl.multiple_of(x * QW, QW), QW), cols], wo_v.at[h, d], sem_wo.at[h * XN + d])
 
     order = [1, XN - 1] + list(range(2, XN - 1))
     later = [functools.partial(lambda i: wq_copy(i).start(), i) for i in range(2, NQ)]
     later += [start_wkv, c_cache[2].start, c_cache[3].start]
     far_first = [2, 1, 3, 0]
-    later += [functools.partial(lambda d: wo_copy(d).start(), d) for d in far_first]
+    later += [functools.partial(lambda h, d: wo_copy(h, d).start(), h, d) for h in range(NH) for d in far_first]
 
     def issue(n):
         for _ in range(n):
@@ -219,11 +219,8 @@
     for i in range(QW // strip):
         sl = slice(i * strip, (i + 1) * strip)
         q_all[x, :, sl] = rope(qb[:, sl], cos_t, sin_lo, sin_hi, half).astype(BF16).astype(F32)
-    qg = []
-    for d in range(1, XN):
-        cp = remote(q_all.at[x], q_all.at[x], s_qg.at[d], r_qg.at[x], xpeer(d))
-        cp.start()
-        qg.append(cp)
+    for d in far_first[:3]:
+        remote(q_all.at[x], q_all.at[x], s_qg.at[0], r_qg.at[0], xpeer(d)).start()
 
     @pl.when(x < XN // 2)
     def _():
@@ -238,15 +235,11 @@
     xkd.start()
     xkd.wait()
     kv_all[x] = kvp[mine, :] + kv_in[...]
-    kg = []
     for d in range(1, XN):
-        cp = remote(kv_all.at[x], kv_all.at[x], s_kg.at[d], r_kg.at[x], xpeer(d))
-        cp.start()
-        kg.append(cp)
-
-    for d in range(XN):
-        if d:
-            remote(q_all.at[x], q_all.at[xs[d]], s_qg.at[d], r_qg.at[xs[d]], xpeer(d)).wait_recv()
+        remote(kv_all.at[x], kv_all.at[x], s_kg.at[0], r_kg.at[0], xpeer(d)).start()
+
+    group = q_all.at[0:XN - 1]
+    remote(group, group, s_qg.at[0], r_qg.at[0], partner).wait_recv()
     for blk in range(XN):
         for j in range(HB):
             h = blk * HB + j
@@ -268,6 +261,7 @@
             s1 = dot(q, k_rcv[b, kv].astype(BF16))
             score[b, kv] = jnp.concatenate([s0, s1], axis=1)
     neg = -jnp.inf
+
     tail_lane = lax.broadcasted_iota(jnp.int32, (G, 128), 1)
     for b in range(BH):
         n = len_s[c * BH + b]
@@ -285,14 +279,11 @@
             ob[0, rows, :] = pv[:, 0:128]
             ob[1, rows, :] = tail
 
-    cr = []
-    for d in range(1, XN):
-        cp = remote(ob.at[:, pl.ds(pl.multiple_of(xs[d] * RB, RB), RB), :], o_in.at[x], s_cr.at[d], r_cr.at[x], xpeer(d))
-        cp.start()
-        cr.append(cp)
-
-    for d in range(1, XN):
-        remote(kv_all.at[x], kv_all.at[xs[d]], s_kg.at[d], r_kg.at[xs[d]], xpeer(d)).wait_recv()
+    for d in far_first[:3]:
+        remote(ob.at[:, pl.ds(pl.multiple_of(xs[d] * RB, RB), RB), :], o_in.at[x], s_cr.at[0], r_cr.at[0], xpeer(d)).start()
+
+    group = kv_all.at[0:XN - 1]
+    remote(group, group, s_kg.at[0], r_kg.at[0], partner).wait_recv()
     kn = kv_all[0]
     vn = kv_all[XN // 2]
     for i in range(1, XN // 2):
@@ -314,8 +305,8 @@
     k_rep = jnp.concatenate([kh] * HB, axis=0)
     v_rep = jnp.concatenate([vh] * HB, axis=0)
     self_s = jnp.sum(q_own * k_rep, axis=1, keepdims=True) * scale
-    for d in range(1, XN):
-        remote(ob.at[:, own, :], o_in.at[xs[d]], s_cr.at[d], r_cr.at[xs[d]], xpeer(d)).wait_recv()
+    group = o_in.at[0:XN - 1]
+    remote(group, group, s_cr.at[0], r_cr.at[0], partner).wait_recv()
     o_in[x] = ob[:, own, :]
     parts = [jnp.concatenate([o_in[i, 0], o_in[i, 1]], axis=1) for i in range(XN)]
     ms = [p[:, HD:HD + 1] for p in parts]
@@ -347,23 +338,30 @@
         cp.start()
         sends.append(cp)
 
-    for d in far_first:
-        wo_copy(d).wait()
-    for h in range(2):
+    for h in range(NH):
         for d in far_first:
-            r = dot(lhs, wo_v[d, :, h * PW:(h + 1) * PW])
-            part[d, 2 * h] = r[0:BH]
-            part[d, 2 * h + 1] = r[BH:]
-            if d:
-                for p in (2 * h, 2 * h + 1):
-                    send(part.at[d, p], p1_in.at[k1, p], s_p1.at[d * NP + p], r_p1.at[k1 * NP + p], along1(d))
+            wo_copy(h, d).wait()
+    for h in range(NH):
+        for d in far_first:
+            r = dot(lhs, wo_v[h, d])
+            for p in (2 * h, 2 * h + 1):
+                part[d, p] = r[(p % 2) * BH:(p % 2 + 1) * BH]
+                if d:
+                    send(part.at[d, p], p1_in.at[k1[h], p], s_p1.at[0], r_p1.at[p], along1(h, d))
+
+    remote(kvn, kv_rcv.at[theirs, :], s_ke.at[0], r_ke.at[0], partner).wait_recv()
+    stores = [pltpu.make_async_copy(kv_rcv.at[:, 0:strip], k_out, sem_small.at[0]),
+              pltpu.make_async_copy(kv_rcv.at[:, strip:2 * strip], v_out, sem_small.at[1])]
+    for cp in stores:
+        cp.start()
 
     for p in range(NP):
-        for d in range(1, XN):
-            remote(part.at[d, p], p1_in.at[k1s[d], p], s_p1.at[d * NP + p], r_p1.at[k1s[d] * NP + p], partner).wait_recv()
-        p2_in[k2, p] = part[0, p] + p1_in[k1s[1], p] + p1_in[k1s[2], p] + p1_in[k1s[3], p]
+        group = p1_in.at[0:XN - 1, p]
+        remote(group, group, s_p1.at[0], r_p1.at[p], partner).wait_recv()
+        h = p // 2
+        p2_in[k2[h], p] = part[0, p] + p1_in[(k1[h] + 1) % XN, p] + p1_in[(k1[h] + 2) % XN, p] + p1_in[(k1[h] + 3) % XN, p]
         for d in order:
-            send(p2_in.at[k2, p], p2_in.at[k2, p], s_p2.at[d * NP + p], r_p2.at[k2 * NP + p], along2(d))
+            send(p2_in.at[k2[h], p], p2_in.at[k2[h], p], s_p2.at[0], r_p2.at[p], along2(h, d))
 
     def place(k, p, cc):
         return (p % 2) * BH, pl.multiple_of(cc * (D // 2) + k * OW + (p // 2) * PW, 128)
@@ -372,63 +370,66 @@
         r0, c0 = place(k, p, cc)
         return og_v.at[r0:r0 + BH, pl.ds(c0, PW)]
 
-    stores = []
-
     def store(i, k, p, cc):
         r0, c0 = place(k, p, cc)
         ob_v[i] = og_v[r0:r0 + BH, pl.ds(c0, PW)].astype(BF16)
-        cp = pltpu.make_async_copy(ob_v.at[i], out.at[r0:r0 + BH, pl.ds(c0, PW)], sem_out.at[i])
+        cp = pltpu.make_async_copy(ob_v.at[i], out.at[r0:r0 + BH, pl.ds(c0, PW)], sem_out.at[0])
         cp.start()
-        stores.append(cp)
 
     for p in range(NP):
-        for d in range(1, XN):
-            remote(part.at[d, p], p2_in.at[k2s[d], p], s_p2.at[d * NP + p], r_p2.at[k2s[d] * NP + p], partner).wait_recv()
-        r0, c0 = place(k1, p, c)
+        group = p2_in.at[0:XN - 1, p]
+        remote(group, group, s_p2.at[0], r_p2.at[p], partner).wait_recv()
+        h = p // 2
+        r0, c0 = place(k1[h], p, c)
         tot = p2_in[0, p] + p2_in[1, p] + p2_in[2, p] + p2_in[3, p]
         res = hid_v[:, pl.ds(c0, PW)].astype(F32)[r0:r0 + BH]
         og_v[r0:r0 + BH, pl.ds(c0, PW)] = (res + tot).astype(BF16).astype(F32)
-        mine_p = view(k1, p, c)
+        mine_p = view(k1[h], p, c)
         for d in order:
-            send(mine_p, mine_p, s_ag.at[d * NP + p], r_ag.at[k1 * NP + p], along1(d))
-        send(mine_p, mine_p, s_of.at[p], r_of.at[k1 * NP + p], partner)
+            send(mine_p, mine_p, s_ag.at[0], r_ag.at[p], along1(h, d))
+        send(mine_p, mine_p, s_of.at[0], r_of.at[p], partner)
     for p in range(NP):
-        store(p, k1, p, c)
+        store(p, k1[p // 2], p, c)
     for p in range(NP):
+        group = p1_in.at[0:XN - 1, p]
+        remote(group, group, s_ag.at[0], r_ag.at[p], partner).wait_recv()
         for d in order:
-            ref = view(k1s[d], p, c)
-            remote(ref, ref, s_ag.at[d * NP + p], r_ag.at[k1s[d] * NP + p], partner).wait_recv()
-            send(ref, ref, s_of.at[d * NP + p], r_of.at[k1s[d] * NP + p], partner)
-            store(d * NP + p, k1s[d], p, c)
-    for d in [0] + order:
-        for p in range(NP):
-            ref = view(k2s[d], p, 1 - c)
-            remote(ref, ref, s_of.at[d * NP + p], r_of.at[k2s[d] * NP + p], partner).wait_recv()
-            store(XN * NP + d * NP + p, k2s[d], p, 1 - c)
-    xe_in = remote(kvn, kv_rcv.at[theirs, :], s_ke.at[0], r_ke.at[0], partner)
-    xe_in.wait_recv()
-    k_out[...] = kv_rcv[:, 0:strip]
-    v_out[...] = kv_rcv[:, strip:2 * strip]
-    for cp in qg + kg + cr + sends:
+            ref = view((k1[p // 2] + d) % XN, p, c)
+            send(ref, ref, s_of.at[0], r_of.at[p], partner)
+        for d in order:
+            store(d * NP + p, (k1[p // 2] + d) % XN, p, c)
+    for p in range(NP):
+        group = p1_in.at[:, p]
+        remote(group, group, s_of.at[0], r_of.at[p], partner).wait_recv()
+        for k in range(XN):
+            store(XN * NP + k * NP + p, k, p, 1 - c)
+    for cp in (xe, cf):
         cp.wait_send()
-    for cp in stores:
+    for group, sem in ((q_all.at[0:XN - 1], s_qg), (kv_all.at[0:XN - 1], s_kg), (o_in.at[0:XN - 1], s_cr), (p1_in.at[0:XN - 1], s_p1),
+                       (p1_in.at[0:XN - 1], s_p2), (p1_in.at[0:XN - 1], s_ag), (p1_in, s_of)):
+        remote(group, group, sem.at[0], r_qg.at[0], partner).wait_send()
+    for cp in stores + [pltpu.make_async_copy(hid_v, out, sem_out.at[0])]:
         cp.wait()
 
 
-def hand_on(o_in, k_in, v_in, o_out, k_out, v_out, buf, s_in, s_out):
+def hand_on(o_in, k_in, v_in, o_out, k_out, v_out, buf, kv_f, kv_b, s_in, s_out):
     n, _, w = buf.shape
     reads = [pltpu.make_async_copy(o_in.at[:, i * w:(i + 1) * w], buf.at[i], s_in.at[i]) for i in range(n)]
     writes = [pltpu.make_async_copy(buf.at[i], o_out.at[:, i * w:(i + 1) * w], s_out.at[i]) for i in range(n)]
-    for r in reads:
+    kv_reads = [pltpu.make_async_copy(src, kv_f.at[i], s_in.at[n + i]) for i, src in enumerate((k_in, v_in))]
+    kv_writes = [pltpu.make_async_copy(kv_b.at[i], dst, s_out.at[n + i]) for i, dst in enumerate((k_out, v_out))]
+    for r in kv_reads + reads:
         r.start()
     hd = k_out.shape[2]
-    for j in range(k_out.shape[1]):
-        k_out[:, j, :] = k_in[:, j * hd:(j + 1) * hd].astype(BF16)
-        v_out[:, j, :] = v_in[:, j * hd:(j + 1) * hd].astype(BF16)
+    for i in range(2):
+        kv_reads[i].wait()
+        for j in range(k_out.shape[1]):
+            kv_b[i, :, j, :] = kv_f[i, :, j * hd:(j + 1) * hd].astype(BF16)
+        kv_writes[i].start()
     for r, w in zip(reads, writes):
         r.wait()
         w.start()
-    for w in writes:
+    for w in kv_writes + writes:
         w.wait()
 
 
@@ -449,7 +450,7 @@
         KVR = KH // (XN // 2)
         HB = QW // HD
         OW = D // SN
-        PW = OW // 2
+        PW = OW // 3
         KW = KVN * HD
         assert w_k.shape[1] == KW and KH % KC == 0 and XN == TN == 4 and KVN == 2
         k_t = jnp.transpose(k_cache, (0, 2, 3, 1))
@@ -460,35 +461,33 @@
         dma = pltpu.SemaphoreType.DMA
         scratch = [
             V((B, D), BF16), V((2, D // 128, 128), BF16), V((2, D // 128, 128), F32), V((B, KH), BF16), pltpu.SMEM((B,), jnp.int32),
-            V((NQ, KC, QW), BF16), V((KVR, KW), BF16), V((XN, QW, OW), BF16),
+            V((NQ, KC, QW), BF16), V((KVR, KW), BF16), V((3, XN, QW, PW), BF16),
             V((B, KVN, HD, SL), BF16), V((B, KVN, HD, SL), BF16),
             V((BH, KVN, HD, SL), F32), V((BH, KVN, HD, SL), F32), V((BH, KVN, HD, SL), F32), V((BH, KVN, HD, SL), F32),
-            V((B, D), F32), V((2 * XN * 4, BH, PW), BF16), V((B, 2 * KW), F32),
+            V((B, D), F32), V((2 * XN * 6, BH, PW), BF16), V((B, 2 * KW), F32),
             V((B, QW), F32), V((BH, QW), F32), V((XN, BH, QW), F32), V((2, XN * HB * BH, 128), F32),
             V((B, KW), F32), V((BH, KW), F32), V((XN, BH, KW), F32), V((BH, 2 * KW), F32),
             V((BH, KVN, G, 2 * SL), F32), V((2, XN * HB * BH, 128), F32), V((XN, 2, HB * BH, 128), F32),
-            V((BH, QW), F32), V((B, QW), F32), V((XN, 4, BH, PW), F32), V((XN, 4, BH, PW), F32), V((XN, 4, BH, PW), F32),
-            dma((4,)), dma((4,)), dma((NQ,)), dma((1,)), dma((XN,)), dma((2 * XN * 4,)),
-            dma((2,)), dma((2,)), dma((1,)), dma((1,)), dma((XN,)), dma((XN,)), dma((1,)), dma((1,)), dma((XN,)), dma((XN,)), dma((1,)), dma((1,)),
-            dma((XN,)), dma((XN,)), dma((1,)), dma((1,)), dma((XN * 4,)), dma((XN * 4,)), dma((XN * 4,)), dma((XN * 4,)),
-            dma((XN * 4,)), dma((XN * 4,)), dma((XN * 4,)), dma((XN * 4,)),
+            V((BH, QW), F32), V((B, QW), F32), V((XN, 6, BH, PW), F32), V((XN, 6, BH, PW), F32), V((XN, 6, BH, PW), F32),
+            dma((4,)), dma((4,)), dma((NQ,)), dma((1,)), dma((3 * XN,)), dma((1,)),
+            dma((2,)), dma((2,)), dma((1,)), dma((1,)), dma((1,)), dma((1,)), dma((1,)), dma((1,)), dma((1,)), dma((1,)), dma((1,)), dma((1,)),
+            dma((1,)), dma((1,)), dma((1,)), dma((1,)), dma((1,)), dma((6,)), dma((1,)), dma((6,)), dma((1,)), dma((6,)), dma((1,)), dma((6,)),
         ]
         cfg = (XN, TN, HD, G, KC, HD ** -0.5)
         out, k_new, v_new = pl.pallas_call(
             functools.partial(kernel, cfg),
             out_shape=(jax.ShapeDtypeStruct((B, D), BF16), jax.ShapeDtypeStruct((B, KW), F32), jax.ShapeDtypeStruct((B, KW), F32)),
             in_specs=[pl.BlockSpec(memory_space=pl.ANY)] * 10,
-            out_specs=(pl.BlockSpec(memory_space=pl.ANY),) + (pl.BlockSpec(memory_space=pltpu.VMEM),) * 2,
+            out_specs=(pl.BlockSpec(memory_space=pl.ANY),) * 3,
             scratch_shapes=scratch,
             compiler_params=pltpu.CompilerParams(collective_id=0, has_side_effects=True, vmem_limit_bytes=67043328),
             name='decode_step',
         )(hidden, gain, bias, w_q, w_k, w_v, w_o, k_t, v_t, lengths)
-        vm = pl.BlockSpec(memory_space=pltpu.VMEM)
         hb = pl.BlockSpec(memory_space=pl.ANY)
         head = jax.ShapeDtypeStruct((B, KVN, HD), BF16)
         return pl.pallas_call(
-            hand_on, out_shape=(jax.ShapeDtypeStruct((B, D), BF16), head, head), in_specs=[hb, vm, vm], out_specs=(hb, vm, vm),
-            scratch_shapes=[V((4, B, D // 4), BF16), dma((4,)), dma((4,))], name='hand_on')(out, k_new, v_new)
+            hand_on, out_shape=(jax.ShapeDtypeStruct((B, D), BF16), head, head), in_specs=[hb] * 3, out_specs=(hb,) * 3,
+            scratch_shapes=[V((2, B, D // 2), BF16), V((2, B, KW), F32), V((2, B, KVN, HD), BF16), dma((4,)), dma((4,))], name='hand_on')(out, k_new, v_new)
 
     row_spec = P('dp', None)
     cache_spec = P('dp', 'sp', 'tp', None)

time: 49.9 us -> 46.7 us (0.936)
  Pallas kernels: 49.1 us -> 45.9 us
    pallas_call x1, Pallas kernels: 45.8 us -> 44 us  [local_step(): pl.pallas_call(functools.partial(kernel, cfg), out_shape=(jax.ShapeDtypeS...]
    pallas_call x1, Pallas kernels: 3.22 us -> 1.88 us  [local_step(): pl.pallas_call(hand_on, out_shape=(jax.ShapeDtypeStruct((B, D), BF16), he...]
where the time goes in v3:
time: 46.7 us; the launch traced here: 46.6 us
  Pallas kernels  45.9 us (98%)
  between operations  0.64 us (1%)
    pallas_call x1, Pallas kernels, local_step(): pl.pallas_call(functools.partial(kernel, cfg), out_shape=(jax.ShapeDtypeS...  44 us
    pallas_call x1, Pallas kernels, local_step(): pl.pallas_call(hand_on, out_shape=(jax.ShapeDtypeStruct((B, D), BF16), he...  1.88 us

profile of v3, /device:TPU:97, one launch (start us, length us, event | category | flops | bytes accessed | tf_op | source)
XLA Modules:
  0.0 46.6 jit_solution(15962526144551974155)
XLA Ops:
  0.6 44.0 %decode_step.1 = (bf16[16,18432]{1,0:T(8,128)(2,1)}, f32[16,384]{1,0:T(8,128)}, f32[16,384]{1,0:T(8,128)}) custom-call(bf16[16,18432]{1,0:T(8,128)(2,1)} %hidden.1, bf16[144,128]{1,0:T(8,128)(2,1)} %bitcast.6, bf16[144,128]{1,0:T(8,128)(2,1)} %bitcast.7, bf16[18432,4608]{1,0:T(8,128)(2,1)} %w_q.1, bf16[18432,384]{1,0:T(8,128)(2,1)} %w_k.1, ...), custom_call_target="tpu_custom_call" | custom-call | tf_op jit(solution)/shard_map/decode_step/pallas_call | solution.py:477
  44.7 1.9 %hand_on.1 = (bf16[16,18432]{1,0:T(8,128)(2,1)}, bf16[16,2,192]{2,1,0:T(2,128)(2,1)}, bf16[16,2,192]{2,1,0:T(2,128)(2,1)}) custom-call(bf16[16,18432]{1,0:T(8,128)(2,1)} %get-tuple-element.6.o_in, f32[16,384]{1,0:T(8,128)} %get-tuple-element.7.k_in, f32[16,384]{1,0:T(8,128)} %get-tuple-element.8.v_in), custom_call_target="tpu_custom_call" | custom-call | tf_op jit(solution)/shard_map/hand_on/pallas_call | solution.py:488
